TPU v7x, 32 devices: a whole 2x2x4 slice. The times are simulated.
32 devices in a mesh: mp: 8 (over z, y), dp: 4 (over x, core).
Axes of the slice: x: 2, y: 2, z: 4, core: 2. Of those that a mesh axis runs over, the one named last changes fastest.
Arguments:
- features: bfloat16 [32, 4, 4, 512], P(('dp', 'mp')), may hold values from 0 to 2
- labels: int32 [32], P('dp'), may hold values from 0 to 9
- subset_ids: int32 [8], P('mp'), may hold values from 0 to 255
- conv1_weight: bfloat16 [8, 9, 512, 512], P('mp'), may hold values from -0.09375 to 0.09375
- conv2_weight: bfloat16 [8, 9, 512, 512], P('mp'), may hold values from -0.09375 to 0.09375
- head_weight: float32 [8, 512, 10], P('mp'), may hold values from -0.25 to 0.25
Outputs:
- datamodel: float32 [32, 256], P(('dp', 'mp'))
- margin_mean: float32 [32], P(('dp', 'mp'))
- margin_norm: float32 [32], P(('dp', 'mp'))
All inputs are finite; a program needn't handle non-finite values.
Results may differ from a plain program's by a relative error of at most 0.00077.
Values may be sent and summed in bfloat16 or wider, within the bound.
A program may use at most 128 MiB of HBM per device.

v0:
```python
import jax
import jax.numpy as jnp
from jax import lax
from jax.sharding import PartitionSpec as P

SUBSETS = 256


def convolve(grid, kernel):
    batch = grid.shape[0]
    width = grid.shape[1]
    chans = grid.shape[3]
    padded = jnp.pad(grid, ((0, 0), (1, 1), (1, 1), (0, 0)))
    result = jnp.zeros((batch * width * width, kernel.shape[2]), jnp.float32)
    for offset in range(9):
        row_off, col_off = divmod(offset, 3)
        shifted = padded[:, row_off : row_off + width, col_off : col_off + width, :].reshape(
            batch * width * width, chans
        )
        result = result + jnp.dot(shifted, kernel[offset], preferred_element_type=jnp.float32)
    return result


def margins_of(grid, first_kernel, second_kernel, head, target_labels):
    batch = grid.shape[0]
    width = grid.shape[1]
    chans = grid.shape[3]
    hidden = (
        jax.nn.relu(convolve(grid, first_kernel))
        .astype(jnp.bfloat16)
        .reshape(batch, width, width, chans)
    )
    branch = jax.nn.relu(convolve(hidden, second_kernel))
    blocked = grid.astype(jnp.float32).reshape(batch * width * width, chans) + branch
    pooled = jnp.max(blocked.reshape(batch, width * width, chans), axis=1)
    logits = jnp.dot(
        pooled, head, precision=lax.Precision.HIGHEST, preferred_element_type=jnp.float32
    )
    classes = jnp.arange(head.shape[1], dtype=jnp.int32)[None, :]
    chosen = classes == target_labels[:, None]
    correct = jnp.sum(jnp.where(chosen, logits, 0.0), axis=1)
    rival = jnp.max(jnp.where(chosen, -1e30, logits), axis=1)
    return correct - rival


def subset_table(identity):
    return (identity[:, None] == jnp.arange(SUBSETS, dtype=jnp.int32)[None, :]).astype(jnp.float32)


def shards(features, labels, subset_ids, conv1_weight, conv2_weight, head_weight):
    models_dev = conv1_weight.shape[0]
    model_count = models_dev * lax.axis_size("mp")
    rows_out = [
        margins_of(
            lax.all_gather(features, "mp", axis=0, tiled=True),
            conv1_weight[0],
            conv2_weight[0],
            head_weight[0],
            labels,
        )
    ]
    margin = jnp.stack(rows_out, 0)
    columns = lax.all_to_all(margin, "mp", split_axis=1, concat_axis=0, tiled=True)
    every_id = lax.all_gather(subset_ids, "mp", axis=0, tiled=True)
    margin_mean = jnp.sum(columns, axis=0) / model_count
    centred = columns - margin_mean[None, :]
    margin_norm = jnp.sqrt(1.0 + jnp.sum(centred * centred, axis=0) / model_count)
    scaled = centred / margin_norm[None, :]
    datamodel = jnp.dot(
        scaled.T,
        subset_table(every_id),
        precision=lax.Precision.HIGHEST,
        preferred_element_type=jnp.float32,
    )
    return (datamodel, margin_mean, margin_norm)


def solution(mesh):
    in_specs = (
        P(("dp", "mp"), None, None, None),
        P("dp"),
        P("mp"),
        P("mp", None, None, None),
        P("mp", None, None, None),
        P("mp", None, None),
    )
    out_specs = (P(("dp", "mp"), None), P(("dp", "mp")), P(("dp", "mp")))
    return jax.shard_map(shards, mesh=mesh, in_specs=in_specs, out_specs=out_specs, check_vma=False)
```

profile of v0, /device:TPU:0, one launch (start us, length us, event | category | flops | bytes accessed | tf_op | source)
XLA Modules:
  0.0 84.1 jit_solution(346595920201907699)
XLA Ops:
  0.6 32.5 %all_gather.6 = bf16[8,4,4,512]{3,2,1,0:T(4,128)(2,1)S(1)} all-gather(bf16[1,4,4,512]{3,2,1,0:T(4,128)(2,1)} %param.6), channel_id=1, replica_groups=mesh['mp'=8,'dp'=4] {'mp'}, dimensions={0}, use_global_device_ids=true | all-gather | bytes 147456 | tf_op jit(solution)/shard_map/all_gather | solution.py:55
  34.0 1.3 %fusion.22 = f32[128,512]{1,0:T(8,128)S(1)} fusion(bf16[128,512]{1,0:T(8,128)(2,1)S(1)} %reshape.174, bf16[1,9,512,512]{3,2,1,0:T(8,128)(2,1)} %param.9), kind=kOutput, calls=%fused_computation.54 | convolution fusion | flops 67108864 | bytes 917504 | tf_op jit(solution)/shard_map/dot_general | solution.py:20
  35.3 1.3 %convolution_add_fusion.15 = f32[128,512]{1,0:T(8,128)S(1)} fusion(f32[128,512]{1,0:T(8,128)S(1)} %fusion.22, bf16[128,512]{1,0:T(8,128)(2,1)S(1)} %reshape.175, bf16[1,9,512,512]{3,2,1,0:T(8,128)(2,1)} %param.9), kind=kOutput, calls=%fused_computation.15 | convolution fusion | flops 67174400 | bytes 1179648 | tf_op jit(solution)/shard_map/dot_general | solution.py:20
  36.6 1.3 %convolution_add_fusion.14 = f32[128,512]{1,0:T(8,128)S(1)} fusion(f32[128,512]{1,0:T(8,128)S(1)} %convolution_add_fusion.15, bf16[128,512]{1,0:T(8,128)(2,1)S(1)} %reshape.176, bf16[1,9,512,512]{3,2,1,0:T(8,128)(2,1)} %param.9), kind=kOutput, calls=%fused_computation.14 | convolution fusion | flops 67174400 | bytes 1179648 | tf_op jit(solution)/shard_map/dot_general | solution.py:20
  37.9 1.3 %convolution_add_fusion.13 = f32[128,512]{1,0:T(8,128)S(1)} fusion(f32[128,512]{1,0:T(8,128)S(1)} %convolution_add_fusion.14, bf16[128,512]{1,0:T(8,128)(2,1)S(1)} %reshape.177, bf16[1,9,512,512]{3,2,1,0:T(8,128)(2,1)} %param.9), kind=kOutput, calls=%fused_computation.13 | convolution fusion | flops 67174400 | bytes 1179648 | tf_op jit(solution)/shard_map/dot_general | solution.py:20
  39.1 1.3 %convolution_add_fusion.12 = f32[128,512]{1,0:T(8,128)S(1)} fusion(f32[128,512]{1,0:T(8,128)S(1)} %convolution_add_fusion.13, bf16[128,512]{1,0:T(8,128)(2,1)S(1)} %reshape.172, bf16[1,9,512,512]{3,2,1,0:T(8,128)(2,1)} %param.9), kind=kOutput, calls=%fused_computation.12 | convolution fusion | flops 67174400 | bytes 1179648 | tf_op jit(solution)/shard_map/dot_general | solution.py:20
  40.4 1.3 %convolution_add_fusion.11 = f32[128,512]{1,0:T(8,128)S(1)} fusion(f32[128,512]{1,0:T(8,128)S(1)} %convolution_add_fusion.12, bf16[128,512]{1,0:T(8,128)(2,1)S(1)} %reshape.178, bf16[1,9,512,512]{3,2,1,0:T(8,128)(2,1)} %param.9), kind=kOutput, calls=%fused_computation.11 | convolution fusion | flops 67174400 | bytes 1179648 | tf_op jit(solution)/shard_map/dot_general | solution.py:20
  41.7 1.3 %convolution_add_fusion.10 = f32[128,512]{1,0:T(8,128)S(1)} fusion(f32[128,512]{1,0:T(8,128)S(1)} %convolution_add_fusion.11, bf16[128,512]{1,0:T(8,128)(2,1)S(1)} %reshape.179, bf16[1,9,512,512]{3,2,1,0:T(8,128)(2,1)} %param.9), kind=kOutput, calls=%fused_computation.10 | convolution fusion | flops 67174400 | bytes 1179648 | tf_op jit(solution)/shard_map/dot_general | solution.py:20
  43.0 1.3 %convolution_add_fusion.9 = f32[128,512]{1,0:T(8,128)S(1)} fusion(f32[128,512]{1,0:T(8,128)S(1)} %convolution_add_fusion.10, bf16[128,512]{1,0:T(8,128)(2,1)S(1)} %reshape.180, bf16[1,9,512,512]{3,2,1,0:T(8,128)(2,1)} %param.9), kind=kOutput, calls=%fused_computation.9 | convolution fusion | flops 67174400 | bytes 1179648 | tf_op jit(solution)/shard_map/dot_general | solution.py:20
  44.3 1.3 %fusion.3 = bf16[128,512]{1,0:T(8,128)(2,1)S(1)} fusion(f32[128,512]{1,0:T(8,128)S(1)} %convolution_add_fusion.9, bf16[128,512]{1,0:T(8,128)(2,1)S(1)} %reshape.181, bf16[1,9,512,512]{3,2,1,0:T(8,128)(2,1)} %param.9), kind=kOutput, calls=%fused_computation.19 | convolution fusion | flops 67305472 | bytes 1048576 | tf_op jit(solution)/shard_map/dot_general | solution.py:20
  46.2 1.3 %fusion.12 = f32[128,512]{1,0:T(8,128)S(1)} fusion(bf16[128,512]{1,0:T(8,128)(2,1)S(1)} %reshape.183, bf16[1,9,512,512]{3,2,1,0:T(8,128)(2,1)} %param.10), kind=kOutput, calls=%fused_computation.44 | convolution fusion | flops 67108864 | bytes 917504 | tf_op jit(solution)/shard_map/dot_general | solution.py:20
  47.5 1.3 %convolution_add_fusion.7 = f32[128,512]{1,0:T(8,128)S(1)} fusion(f32[128,512]{1,0:T(8,128)S(1)} %fusion.12, bf16[128,512]{1,0:T(8,128)(2,1)S(1)} %reshape.184, bf16[1,9,512,512]{3,2,1,0:T(8,128)(2,1)} %param.10), kind=kOutput, calls=%fused_computation.7 | convolution fusion | flops 67174400 | bytes 1179648 | tf_op jit(solution)/shard_map/dot_general | solution.py:20
  48.8 1.3 %convolution_add_fusion.6 = f32[128,512]{1,0:T(8,128)S(1)} fusion(f32[128,512]{1,0:T(8,128)S(1)} %convolution_add_fusion.7, bf16[128,512]{1,0:T(8,128)(2,1)S(1)} %reshape.185, bf16[1,9,512,512]{3,2,1,0:T(8,128)(2,1)} %param.10), kind=kOutput, calls=%fused_computation.6 | convolution fusion | flops 67174400 | bytes 1179648 | tf_op jit(solution)/shard_map/dot_general | solution.py:20
  50.1 1.3 %convolution_add_fusion.5 = f32[128,512]{1,0:T(8,128)S(1)} fusion(f32[128,512]{1,0:T(8,128)S(1)} %convolution_add_fusion.6, bf16[128,512]{1,0:T(8,128)(2,1)S(1)} %reshape.186, bf16[1,9,512,512]{3,2,1,0:T(8,128)(2,1)} %param.10), kind=kOutput, calls=%fused_computation.5 | convolution fusion | flops 67174400 | bytes 1179648 | tf_op jit(solution)/shard_map/dot_general | solution.py:20
  51.4 1.3 %convolution_add_fusion.4 = f32[128,512]{1,0:T(8,128)S(1)} fusion(f32[128,512]{1,0:T(8,128)S(1)} %convolution_add_fusion.5, bf16[128,512]{1,0:T(8,128)(2,1)S(1)} %fusion.3, bf16[1,9,512,512]{3,2,1,0:T(8,128)(2,1)} %param.10), kind=kOutput, calls=%fused_computation.4 | convolution fusion | flops 67174400 | bytes 1179648 | tf_op jit(solution)/shard_map/dot_general | solution.py:20
  52.8 1.3 %convolution_add_fusion.3 = f32[128,512]{1,0:T(8,128)S(1)} fusion(f32[128,512]{1,0:T(8,128)S(1)} %convolution_add_fusion.4, bf16[128,512]{1,0:T(8,128)(2,1)S(1)} %reshape.187, bf16[1,9,512,512]{3,2,1,0:T(8,128)(2,1)} %param.10), kind=kOutput, calls=%fused_computation.3 | convolution fusion | flops 67174400 | bytes 1179648 | tf_op jit(solution)/shard_map/dot_general | solution.py:20
  54.1 1.3 %convolution_add_fusion.2 = f32[128,512]{1,0:T(8,128)S(1)} fusion(f32[128,512]{1,0:T(8,128)S(1)} %convolution_add_fusion.3, bf16[128,512]{1,0:T(8,128)(2,1)S(1)} %reshape.188, bf16[1,9,512,512]{3,2,1,0:T(8,128)(2,1)} %param.10), kind=kOutput, calls=%fused_computation.2 | convolution fusion | flops 67174400 | bytes 1179648 | tf_op jit(solution)/shard_map/dot_general | solution.py:20
  55.4 1.3 %convolution_add_fusion.1 = f32[128,512]{1,0:T(8,128)S(1)} fusion(f32[128,512]{1,0:T(8,128)S(1)} %convolution_add_fusion.2, bf16[128,512]{1,0:T(8,128)(2,1)S(1)} %reshape.189, bf16[1,9,512,512]{3,2,1,0:T(8,128)(2,1)} %param.10), kind=kOutput, calls=%fused_computation.1 | convolution fusion | flops 67174400 | bytes 1179648 | tf_op jit(solution)/shard_map/dot_general | solution.py:20
  56.7 1.3 %bitcast_reduce_fusion = f32[8,512]{1,0:T(8,128)S(1)} fusion(f32[128,512]{1,0:T(8,128)S(1)} %convolution_add_fusion.1, bf16[128,512]{1,0:T(8,128)(2,1)S(1)} %reshape.190, bf16[1,9,512,512]{3,2,1,0:T(8,128)(2,1)} %param.10, bf16[128,512]{1,0:T(8,128)(2,1)S(1)} %reshape.172), kind=kOutput, calls=%fused_computation.74 | convolution fusion | flops 67432448 | bytes 1064960 | tf_op jit(solution)/shard_map/dot_general | solution.py:20
  58.3 0.7 copy.10
  60.2 0.8 dynamic-update-slice
  61.0 5.5 %all-to-all-start = ((f32[1,8,1]{2,0,1:T(1,128)}), f32[1,8,1]{2,0,1:T(1,128)S(1)}, u32[]{:S(2)}, u32[]{:S(2)}) async-start(f32[1,8,1]{2,0,1:T(1,128)} %copy.10), calls=%async_computation | async-start | bytes 8192 | tf_op jit(solution)/shard_map/all_to_all | solution.py:63
  66.5 11.9 %all-reduce.2 = s32[8]{0:T(128)S(1)} all-reduce(s32[8]{0:T(128)S(1)} %dynamic-update-slice), channel_id=1, replica_groups=mesh['mp'=8,'dp'=4] {'mp'}, use_global_device_ids=true, to_apply=%add.2 | all-reduce | flops 8 | bytes 64
  81.1 0.8 fusion.47
  (34 shorter events, 3.9 us)
Async XLA Ops:
  48.8 9.2 %copy-start = (f32[1,512,10]{1,0,2:T(1,128)S(1)}, f32[1,512,10]{1,0,2:T(1,128)}, u32[]{:S(2)}) copy-start(f32[1,512,10]{1,0,2:T(1,128)} %param.11) | copy-start | bytes 61444
  48.8 9.2 %copy-start.1 = (s32[8]{0:T(128)S(1)}, s32[8]{0:T(128)}, u32[]{:S(2)}) copy-start(s32[8]{0:T(128)} %param.7) | copy-start | bytes 100
  48.8 10.8 %copy-start.2 = (u32[32]{0:T(128)S(1)}, u32[32]{0:T(128)}, u32[]{:S(2)}) copy-start(u32[32]{0:T(128)} %constant.32) | copy-start | bytes 388
  61.0 17.4 %all-to-all-start = ((f32[1,8,1]{2,0,1:T(1,128)}), f32[1,8,1]{2,0,1:T(1,128)S(1)}, u32[]{:S(2)}, u32[]{:S(2)}) async-start(f32[1,8,1]{2,0,1:T(1,128)} %copy.10), calls=%async_computation | async-start | bytes 8192 | tf_op jit(solution)/shard_map/all_to_all | solution.py:63
where the time goes:
time: 85.2 us; the launch traced here: 84.1 us
  blocking collectives  44.4 us (52%)
  matrix products  24 us (28%)
  starting transfers between devices  5.52 us (6%)
  between operations  5.14 us (6%)
  local copies, waits for them, and re-layouts  3.67 us (4%)
  other arithmetic  1.37 us (2%)
    all_gather x1, blocking collectives, shards(): lax.all_gather(features, 'mp', axis=0, tiled=True)  32.5 us
    dot_general x18, matrix products, convolve(): jnp.dot(shifted, kernel[offset], preferred_element_type=jnp.float32)  23 us
    unnamed x1, blocking collectives  11.9 us
    all_to_all x1, starting transfers between devices, shards(): lax.all_to_all(margin, 'mp', split_axis=1, concat_axis=0, tiled=True)  5.52 us
  transfers between devices with their start and end apart: 1, of which 0 were waited for; matrix products, arithmetic and copies ran while one was open for 0% of the time, Pallas kernels for 0%

commit v1 on v0

--- a/solution.py
+++ b/solution.py
@@ -60,7 +60,10 @@
         )
     ]
     margin = jnp.stack(rows_out, 0)
-    columns = lax.all_to_all(margin, "mp", split_axis=1, concat_axis=0, tiled=True)
+    columns = jnp.concatenate(
+        lax.all_to_all(jnp.stack(jnp.split(margin, lax.axis_size("mp"), axis=1)), "mp", 0, 0),
+        axis=0,
+    )
     every_id = lax.all_gather(subset_ids, "mp", axis=0, tiled=True)
     margin_mean = jnp.sum(columns, axis=0) / model_count
     centred = columns - margin_mean[None, :]

time: 85.2 us -> 94.6 us (1.11)
  local copies, waits for them, and re-layouts: 3.67 us -> 13 us
    unnamed x9 -> x16, local copies, waits for them, and re-layouts: 1.36 us -> 9.54 us
    another operation x0 -> x1, local copies, waits for them, and re-layouts: none -> 1.17 us  [shards(): jnp.stack(jnp.split(margin, lax.axis_size('mp'), axis=1))]
where the time goes in v1:
time: 94.6 us; the launch traced here: 93.4 us
  blocking collectives  44.4 us (47%)
  matrix products  24 us (25%)
  local copies, waits for them, and re-layouts  13 us (14%)
  starting transfers between devices  5.52 us (6%)
  between operations  5.13 us (5%)
  other arithmetic  1.37 us (1%)
    all_gather x1, blocking collectives, shards(): lax.all_gather(features, 'mp', axis=0, tiled=True)  32.5 us
    dot_general x18, matrix products, convolve(): jnp.dot(shifted, kernel[offset], preferred_element_type=jnp.float32)  23 us
    unnamed x1, blocking collectives  11.9 us
    unnamed x16, local copies, waits for them, and re-layouts  9.54 us
    all_to_all x1, starting transfers between devices, shards(): lax.all_to_all(jnp.stack(jnp.split(margin, lax.axis_size('mp'), axis=1)),...  5.52 us
  transfers between devices with their start and end apart: 1, of which 0 were waited for; matrix products, arithmetic and copies ran while one was open for 0% of the time, Pallas kernels for 0%

profile of v1, /device:TPU:0, one launch (start us, length us, event | category | flops | bytes accessed | tf_op | source)
XLA Modules:
  0.0 93.4 jit_solution(11981454319280243044)
XLA Ops:
  0.6 32.5 %all_gather.6 = bf16[8,4,4,512]{3,2,1,0:T(4,128)(2,1)S(1)} all-gather(bf16[1,4,4,512]{3,2,1,0:T(4,128)(2,1)} %param.6), channel_id=1, replica_groups=mesh['mp'=8,'dp'=4] {'mp'}, dimensions={0}, use_global_device_ids=true | all-gather | bytes 147456 | tf_op jit(solution)/shard_map/all_gather | solution.py:55
  34.0 1.3 %fusion.22 = f32[128,512]{1,0:T(8,128)S(1)} fusion(bf16[128,512]{1,0:T(8,128)(2,1)S(1)} %reshape.168, bf16[1,9,512,512]{3,2,1,0:T(8,128)(2,1)} %param.9), kind=kOutput, calls=%fused_computation.54 | convolution fusion | flops 67108864 | bytes 917504 | tf_op jit(solution)/shard_map/dot_general | solution.py:20
  35.3 1.3 %convolution_add_fusion.15 = f32[128,512]{1,0:T(8,128)S(1)} fusion(f32[128,512]{1,0:T(8,128)S(1)} %fusion.22, bf16[128,512]{1,0:T(8,128)(2,1)S(1)} %reshape.169, bf16[1,9,512,512]{3,2,1,0:T(8,128)(2,1)} %param.9), kind=kOutput, calls=%fused_computation.15 | convolution fusion | flops 67174400 | bytes 1179648 | tf_op jit(solution)/shard_map/dot_general | solution.py:20
  36.6 1.3 %convolution_add_fusion.14 = f32[128,512]{1,0:T(8,128)S(1)} fusion(f32[128,512]{1,0:T(8,128)S(1)} %convolution_add_fusion.15, bf16[128,512]{1,0:T(8,128)(2,1)S(1)} %reshape.170, bf16[1,9,512,512]{3,2,1,0:T(8,128)(2,1)} %param.9), kind=kOutput, calls=%fused_computation.14 | convolution fusion | flops 67174400 | bytes 1179648 | tf_op jit(solution)/shard_map/dot_general | solution.py:20
  37.9 1.3 %convolution_add_fusion.13 = f32[128,512]{1,0:T(8,128)S(1)} fusion(f32[128,512]{1,0:T(8,128)S(1)} %convolution_add_fusion.14, bf16[128,512]{1,0:T(8,128)(2,1)S(1)} %reshape.171, bf16[1,9,512,512]{3,2,1,0:T(8,128)(2,1)} %param.9), kind=kOutput, calls=%fused_computation.13 | convolution fusion | flops 67174400 | bytes 1179648 | tf_op jit(solution)/shard_map/dot_general | solution.py:20
  39.1 1.3 %convolution_add_fusion.12 = f32[128,512]{1,0:T(8,128)S(1)} fusion(f32[128,512]{1,0:T(8,128)S(1)} %convolution_add_fusion.13, bf16[128,512]{1,0:T(8,128)(2,1)S(1)} %reshape.166, bf16[1,9,512,512]{3,2,1,0:T(8,128)(2,1)} %param.9), kind=kOutput, calls=%fused_computation.12 | convolution fusion | flops 67174400 | bytes 1179648 | tf_op jit(solution)/shard_map/dot_general | solution.py:20
  40.4 1.3 %convolution_add_fusion.11 = f32[128,512]{1,0:T(8,128)S(1)} fusion(f32[128,512]{1,0:T(8,128)S(1)} %convolution_add_fusion.12, bf16[128,512]{1,0:T(8,128)(2,1)S(1)} %reshape.172, bf16[1,9,512,512]{3,2,1,0:T(8,128)(2,1)} %param.9), kind=kOutput, calls=%fused_computation.11 | convolution fusion | flops 67174400 | bytes 1179648 | tf_op jit(solution)/shard_map/dot_general | solution.py:20
  41.7 1.3 %convolution_add_fusion.10 = f32[128,512]{1,0:T(8,128)S(1)} fusion(f32[128,512]{1,0:T(8,128)S(1)} %convolution_add_fusion.11, bf16[128,512]{1,0:T(8,128)(2,1)S(1)} %reshape.173, bf16[1,9,512,512]{3,2,1,0:T(8,128)(2,1)} %param.9), kind=kOutput, calls=%fused_computation.10 | convolution fusion | flops 67174400 | bytes 1179648 | tf_op jit(solution)/shard_map/dot_general | solution.py:20
  43.0 1.3 %convolution_add_fusion.9 = f32[128,512]{1,0:T(8,128)S(1)} fusion(f32[128,512]{1,0:T(8,128)S(1)} %convolution_add_fusion.10, bf16[128,512]{1,0:T(8,128)(2,1)S(1)} %reshape.174, bf16[1,9,512,512]{3,2,1,0:T(8,128)(2,1)} %param.9), kind=kOutput, calls=%fused_computation.9 | convolution fusion | flops 67174400 | bytes 1179648 | tf_op jit(solution)/shard_map/dot_general | solution.py:20
  44.3 1.3 %fusion.3 = bf16[128,512]{1,0:T(8,128)(2,1)S(1)} fusion(f32[128,512]{1,0:T(8,128)S(1)} %convolution_add_fusion.9, bf16[128,512]{1,0:T(8,128)(2,1)S(1)} %reshape.175, bf16[1,9,512,512]{3,2,1,0:T(8,128)(2,1)} %param.9), kind=kOutput, calls=%fused_computation.19 | convolution fusion | flops 67305472 | bytes 1048576 | tf_op jit(solution)/shard_map/dot_general | solution.py:20
  46.2 1.3 %fusion.12 = f32[128,512]{1,0:T(8,128)S(1)} fusion(bf16[128,512]{1,0:T(8,128)(2,1)S(1)} %reshape.177, bf16[1,9,512,512]{3,2,1,0:T(8,128)(2,1)} %param.10), kind=kOutput, calls=%fused_computation.44 | convolution fusion | flops 67108864 | bytes 917504 | tf_op jit(solution)/shard_map/dot_general | solution.py:20
  47.5 1.3 %convolution_add_fusion.7 = f32[128,512]{1,0:T(8,128)S(1)} fusion(f32[128,512]{1,0:T(8,128)S(1)} %fusion.12, bf16[128,512]{1,0:T(8,128)(2,1)S(1)} %reshape.178, bf16[1,9,512,512]{3,2,1,0:T(8,128)(2,1)} %param.10), kind=kOutput, calls=%fused_computation.7 | convolution fusion | flops 67174400 | bytes 1179648 | tf_op jit(solution)/shard_map/dot_general | solution.py:20
  48.8 1.3 %convolution_add_fusion.6 = f32[128,512]{1,0:T(8,128)S(1)} fusion(f32[128,512]{1,0:T(8,128)S(1)} %convolution_add_fusion.7, bf16[128,512]{1,0:T(8,128)(2,1)S(1)} %reshape.179, bf16[1,9,512,512]{3,2,1,0:T(8,128)(2,1)} %param.10), kind=kOutput, calls=%fused_computation.6 | convolution fusion | flops 67174400 | bytes 1179648 | tf_op jit(solution)/shard_map/dot_general | solution.py:20
  50.1 1.3 %convolution_add_fusion.5 = f32[128,512]{1,0:T(8,128)S(1)} fusion(f32[128,512]{1,0:T(8,128)S(1)} %convolution_add_fusion.6, bf16[128,512]{1,0:T(8,128)(2,1)S(1)} %reshape.180, bf16[1,9,512,512]{3,2,1,0:T(8,128)(2,1)} %param.10), kind=kOutput, calls=%fused_computation.5 | convolution fusion | flops 67174400 | bytes 1179648 | tf_op jit(solution)/shard_map/dot_general | solution.py:20
  51.4 1.3 %convolution_add_fusion.4 = f32[128,512]{1,0:T(8,128)S(1)} fusion(f32[128,512]{1,0:T(8,128)S(1)} %convolution_add_fusion.5, bf16[128,512]{1,0:T(8,128)(2,1)S(1)} %fusion.3, bf16[1,9,512,512]{3,2,1,0:T(8,128)(2,1)} %param.10), kind=kOutput, calls=%fused_computation.4 | convolution fusion | flops 67174400 | bytes 1179648 | tf_op jit(solution)/shard_map/dot_general | solution.py:20
  52.8 1.3 %convolution_add_fusion.3 = f32[128,512]{1,0:T(8,128)S(1)} fusion(f32[128,512]{1,0:T(8,128)S(1)} %convolution_add_fusion.4, bf16[128,512]{1,0:T(8,128)(2,1)S(1)} %reshape.181, bf16[1,9,512,512]{3,2,1,0:T(8,128)(2,1)} %param.10), kind=kOutput, calls=%fused_computation.3 | convolution fusion | flops 67174400 | bytes 1179648 | tf_op jit(solution)/shard_map/dot_general | solution.py:20
  54.1 1.3 %convolution_add_fusion.2 = f32[128,512]{1,0:T(8,128)S(1)} fusion(f32[128,512]{1,0:T(8,128)S(1)} %convolution_add_fusion.3, bf16[128,512]{1,0:T(8,128)(2,1)S(1)} %reshape.182, bf16[1,9,512,512]{3,2,1,0:T(8,128)(2,1)} %param.10), kind=kOutput, calls=%fused_computation.2 | convolution fusion | flops 67174400 | bytes 1179648 | tf_op jit(solution)/shard_map/dot_general | solution.py:20
  55.4 1.3 %convolution_add_fusion.1 = f32[128,512]{1,0:T(8,128)S(1)} fusion(f32[128,512]{1,0:T(8,128)S(1)} %convolution_add_fusion.2, bf16[128,512]{1,0:T(8,128)(2,1)S(1)} %reshape.183, bf16[1,9,512,512]{3,2,1,0:T(8,128)(2,1)} %param.10), kind=kOutput, calls=%fused_computation.1 | convolution fusion | flops 67174400 | bytes 1179648 | tf_op jit(solution)/shard_map/dot_general | solution.py:20
  56.7 1.3 %bitcast_reduce_fusion = f32[8,512]{1,0:T(8,128)S(1)} fusion(f32[128,512]{1,0:T(8,128)S(1)} %convolution_add_fusion.1, bf16[128,512]{1,0:T(8,128)(2,1)S(1)} %reshape.184, bf16[1,9,512,512]{3,2,1,0:T(8,128)(2,1)} %param.10, bf16[128,512]{1,0:T(8,128)(2,1)S(1)} %reshape.166), kind=kOutput, calls=%fused_computation.74 | convolution fusion | flops 67432448 | bytes 1064960 | tf_op jit(solution)/shard_map/dot_general | solution.py:20
  63.1 1.2 %constant_dynamic-update-slice_fusion.4 = f32[8,1,1]{2,1,0:T(1,128)} fusion(f32[8,1,1]{2,1,0:T(1,128)} %constant_dynamic-update-slice_fusion.5, f32[1,1,1]{2,1,0:T(1,128)} %bitcast.23), kind=kLoop, calls=%fused_computation.82 | loop fusion | bytes 1024
  65.4 1.2 %constant_dynamic-update-slice_fusion.2 = f32[8,1,1]{2,1,0:T(1,128)} fusion(f32[8,1,1]{2,1,0:T(1,128)} %constant_dynamic-update-slice_fusion.3, f32[1,1,1]{2,1,0:T(1,128)} %bitcast.25), kind=kLoop, calls=%fused_computation.80 | loop fusion | bytes 1024
  66.6 1.2 %constant_dynamic-update-slice_fusion.1 = f32[8,1,1]{2,1,0:T(1,128)} fusion(f32[8,1,1]{2,1,0:T(1,128)} %constant_dynamic-update-slice_fusion.2, f32[1,1,1]{2,1,0:T(1,128)} %bitcast.26), kind=kLoop, calls=%fused_computation.79 | loop fusion | bytes 1024
  70.3 5.5 %all-to-all-start = ((f32[8,1,1]{2,1,0:T(1,128)}), f32[8,1,1]{2,1,0:T(1,128)S(1)}, u32[]{:S(2)}, u32[]{:S(2)}) async-start(f32[8,1,1]{2,1,0:T(1,128)} %constant_dynamic-update-slice_fusion), calls=%async_computation | async-start | bytes 8192 | tf_op jit(solution)/shard_map/all_to_all | solution.py:64
  75.8 11.9 %all-reduce.2 = s32[8]{0:T(128)S(1)} all-reduce(s32[8]{0:T(128)S(1)} %dynamic-update-slice), channel_id=1, replica_groups=mesh['mp'=8,'dp'=4] {'mp'}, use_global_device_ids=true, to_apply=%add.2 | all-reduce | flops 8 | bytes 64
  (42 shorter events, 11.7 us)
Async XLA Ops:
  48.8 9.2 %copy-start = (f32[1,512,10]{1,0,2:T(1,128)S(1)}, f32[1,512,10]{1,0,2:T(1,128)}, u32[]{:S(2)}) copy-start(f32[1,512,10]{1,0,2:T(1,128)} %param.11) | copy-start | bytes 61444
  48.8 9.2 %copy-start.1 = (s32[8]{0:T(128)S(1)}, s32[8]{0:T(128)}, u32[]{:S(2)}) copy-start(s32[8]{0:T(128)} %param.7) | copy-start | bytes 100
  48.8 20.1 %copy-start.2 = (u32[32]{0:T(128)S(1)}, u32[32]{0:T(128)}, u32[]{:S(2)}) copy-start(u32[32]{0:T(128)} %constant.32) | copy-start | bytes 388
  70.3 17.4 %all-to-all-start = ((f32[8,1,1]{2,1,0:T(1,128)}), f32[8,1,1]{2,1,0:T(1,128)S(1)}, u32[]{:S(2)}, u32[]{:S(2)}) async-start(f32[8,1,1]{2,1,0:T(1,128)} %constant_dynamic-update-slice_fusion), calls=%async_computation | async-start | bytes 8192 | tf_op jit(solution)/shard_map/all_to_all | solution.py:64
